TPU v7x, 256 devices: a whole 4x4x8 slice. The times are simulated.
256 devices in a mesh: outer: 16 (over z_lo, x), inner: 16 (over y, z_hi, core).
Axes of the slice: x: 4, y: 4, z: 8 (z_hi: 2, z_lo: 4; z = z_hi * 4 + z_lo), core: 2. Of those that a mesh axis runs over, the one named last changes fastest.
Arguments:
- queries: bfloat16 [8192, 2, 4096], P('outer', None, 'inner'), may hold values from -52 to 52
- keys: bfloat16 [8192, 2, 4096], P('outer', None, 'inner'), may hold values from -6 to 6
- values: bfloat16 [8192, 2, 4096], P('outer', None, 'inner'), may hold values from -6 to 6
Outputs:
- attended: bfloat16 [8192, 2, 4096], P(('outer', 'inner'))
All inputs are finite; a program needn't handle non-finite values.
Results may differ from a plain program's by a relative error of at most 0.004.
Values may be sent and summed in bfloat16 or wider, within the bound.
A program may use at most 128 MiB of HBM per device.

v0:
```python
from functools import partial
import math
import jax
import jax.numpy as jnp
from jax import lax
from jax.sharding import PartitionSpec as P

HEAD_DIM = 128


def attend_keys(running, key_block, value_block, query_heads, head_count):
    peak_rows, totals, numerator = running
    key_count = key_block.shape[0]
    key_heads = key_block.reshape(key_count, head_count, HEAD_DIM)
    value_heads = value_block.reshape(key_count, head_count, HEAD_DIM)
    scores = jnp.einsum(
        "qhd,khd->qhk", query_heads, key_heads, preferred_element_type=jnp.float32
    ) * (1.0 / math.sqrt(HEAD_DIM))
    new_peaks = jnp.maximum(peak_rows, jnp.max(scores, axis=2))
    shrink = jnp.exp(peak_rows - new_peaks)
    weights = jnp.exp(scores - new_peaks[..., None])
    totals = totals * shrink + jnp.sum(weights, axis=2)
    numerator = numerator * shrink[..., None] + jnp.einsum(
        "qhk,khd->qhd",
        weights.astype(jnp.bfloat16),
        value_heads,
        preferred_element_type=jnp.float32,
    )
    return (new_peaks, totals, numerator)


def attend_piece(running, pieces, start_row, query_part, head_count):
    key_rows, value_rows = pieces
    row_count = query_part.shape[0]
    query_heads = query_part.reshape(row_count, head_count, HEAD_DIM)
    block_count = key_rows.shape[0] // row_count
    key_blocks = key_rows.reshape(block_count, row_count, key_rows.shape[1])
    value_blocks = value_rows.reshape(block_count, row_count, value_rows.shape[1])

    def one_block(state, blocks):
        return (attend_keys(state, blocks[0], blocks[1], query_heads, head_count), None)

    running, unused = lax.scan(one_block, running, (key_blocks, value_blocks))
    return running


def start_state(row_count, head_count):
    peak_rows = jnp.full((row_count, head_count), -1e30, jnp.float32)
    totals = jnp.zeros((row_count, head_count), jnp.float32)
    numerator = jnp.zeros((row_count, head_count, HEAD_DIM), jnp.float32)
    return (peak_rows, totals, numerator)


def finish_state(running):
    peak_rows, totals, numerator = running
    averaged = numerator / totals[..., None]
    return averaged.reshape(numerator.shape[0], -1).astype(jnp.bfloat16)


def flatten(array):
    return array.reshape(array.shape[0], array.shape[1] * array.shape[2])


def per_device(queries, keys, values):
    tok_rows, networks, local_cols = queries.shape
    flat_queries, flat_keys, flat_values = (flatten(queries), flatten(keys), flatten(values))
    head_count = networks * local_cols // HEAD_DIM
    folder = partial(attend_piece, query_part=flat_queries, head_count=head_count)
    running = folder(
        start_state(tok_rows, head_count),
        (
            lax.all_gather(flat_keys, "outer", axis=0, tiled=True),
            lax.all_gather(flat_values, "outer", axis=0, tiled=True),
        ),
        jnp.int32(0),
    )
    local_out = finish_state(running).reshape(tok_rows, networks, local_cols)
    attended = lax.all_to_all(local_out, "inner", split_axis=0, concat_axis=2, tiled=True)
    return attended


def solution(mesh):
    return jax.shard_map(
        per_device,
        mesh=mesh,
        in_specs=(P("outer", None, "inner"), P("outer", None, "inner"), P("outer", None, "inner")),
        out_specs=P(("outer", "inner"), None, None),
        check_vma=False,
    )
```

profile of v0, /device:TPU:32, one launch (start us, length us, event | category | flops | bytes accessed | tf_op | source)
XLA Modules:
  0.0 320.9 jit_solution(2837683536750189921)
XLA Ops:
  6.5 1.9 copy.35
  8.5 1.9 copy.36
  10.5 1.3 copy.21
  12.1 99.0 %all-gather.3.cloned.1.call-done = bf16[8192,512]{1,0:T(8,128)(2,1)} async-done(((bf16[512,512]{1,0:T(8,128)(2,1)}), bf16[8192,512]{1,0:T(8,128)(2,1)}) %all-gather.3.cloned.1.call-update) | async-done | bytes 8388624 | tf_op jit(solution)/shard_map/all_gather | solution.py:72
  111.1 101.0 %all-gather.5.cloned.1.call-done = bf16[8192,512]{1,0:T(8,128)(2,1)} async-done(((bf16[512,512]{1,0:T(8,128)(2,1)}), bf16[8192,512]{1,0:T(8,128)(2,1)}) %all-gather.5.cloned.1.call-update) | async-done | bytes 8388624 | tf_op jit(solution)/shard_map/all_gather | solution.py:73
  212.0 70.4 %while.15 = (s32[]{:T(128)}, f32[512,4]{0,1:T(4,128)S(1)}, f32[512,4]{0,1:T(4,128)S(1)}, f32[512,4,128]{0,2,1:T(8,128)S(1)}, bf16[16,512,512]{2,1,0:T(8,128)(2,1...) while((s32[]{:T(128)}, f32[512,4]{0,1:T(4,128)S(1)}, ...), condition=%wide.region_3.4_spmd.clone, body=%wide.region_0.3_spmd.clone.sunk | while | flops 546056192 | bytes 20578420 | solution.py:43
  212.0 1.3 constant_dynamic-slice_fusion.3
  213.7 0.8 bitcast_reduce_fusion.2
  214.5 0.7 fusion.29
  215.2 1.1 fusion.31
  216.4 1.3 constant_dynamic-slice_fusion.3
  218.1 0.8 bitcast_reduce_fusion.2
  218.9 0.7 fusion.29
  219.6 1.1 fusion.31
  220.8 1.3 constant_dynamic-slice_fusion.3
  222.5 0.8 bitcast_reduce_fusion.2
  223.3 0.7 fusion.29
  224.1 1.1 fusion.31
  225.2 1.3 constant_dynamic-slice_fusion.3
  226.9 0.8 bitcast_reduce_fusion.2
  227.7 0.7 fusion.29
  228.5 1.1 fusion.31
  229.6 1.3 constant_dynamic-slice_fusion.3
  231.3 0.8 bitcast_reduce_fusion.2
  232.1 0.7 fusion.29
  232.9 1.1 fusion.31
  234.0 1.3 constant_dynamic-slice_fusion.3
  235.7 0.8 bitcast_reduce_fusion.2
  237.3 1.1 fusion.31
  238.4 1.3 constant_dynamic-slice_fusion.3
  240.2 0.8 bitcast_reduce_fusion.2
  240.9 0.7 fusion.29
  241.7 1.1 fusion.31
  242.8 1.3 constant_dynamic-slice_fusion.3
  244.6 0.8 bitcast_reduce_fusion.2
  246.1 1.1 fusion.31
  247.3 1.3 constant_dynamic-slice_fusion.3
  249.0 0.8 bitcast_reduce_fusion.2
  249.7 0.7 fusion.29
  250.5 1.1 fusion.31
  251.7 1.3 constant_dynamic-slice_fusion.3
  253.4 0.8 bitcast_reduce_fusion.2
  254.9 1.1 fusion.31
  256.1 1.3 constant_dynamic-slice_fusion.3
  257.8 0.8 bitcast_reduce_fusion.2
  258.6 0.7 fusion.29
  259.3 1.1 fusion.31
  260.5 1.3 constant_dynamic-slice_fusion.3
  262.2 0.8 bitcast_reduce_fusion.2
  263.7 1.1 fusion.31
  264.9 1.3 constant_dynamic-slice_fusion.3
  266.6 0.8 bitcast_reduce_fusion.2
  268.1 1.1 fusion.31
  269.3 1.3 constant_dynamic-slice_fusion.3
  271.0 0.8 bitcast_reduce_fusion.2
  272.5 1.1 fusion.31
  273.7 1.3 constant_dynamic-slice_fusion.3
  275.4 0.8 bitcast_reduce_fusion.2
  276.9 1.1 fusion.31
  278.1 1.3 constant_dynamic-slice_fusion.3
  279.8 0.8 bitcast_reduce_fusion.2
  281.3 1.1 fusion.31
  283.1 29.7 %all_to_all.18 = bf16[512,2,256]{2,1,0:T(2,128)(2,1)S(1)} all-to-all(bf16[512,2,256]{2,1,0:T(2,128)(2,1)S(1)} %copy.25), channel_id=1, replica_groups=mesh['outer'=16,'inner'=16] {'inner'}, dimensions={0} | all-to-all | bytes 1048576 | tf_op jit(solution)/shard_map/all_to_all | solution.py:78
  313.2 0.9 reshape.33
  (100 shorter events, 14.3 us)
Async XLA Ops:
  6.5 104.5 %all-gather.3.cloned.1.call-start = ((), (), s32[]{:S(2)}) async-start(), calls=%async_computation.1 | async-start | bytes 8912896 | tf_op jit(solution)/shard_map/all_gather | solution.py:72
  8.5 203.5 %all-gather.5.cloned.1.call-start = ((), (), s32[]{:S(2)}) async-start(), calls=%async_computation.2 | async-start | bytes 8912896 | tf_op jit(solution)/shard_map/all_gather | solution.py:73
Sparse Core Ops, SparseCore 0:
  9.1 101.9 all-gather.2
  112.9 99.1 all-gather.4
where the time goes:
time: 322 us; the launch traced here: 321 us
  waiting for transfers between devices  200 us (62%)
  local copies, waits for them, and re-layouts  34.4 us (11%)
  matrix products  30.6 us (10%)
  blocking collectives  29.7 us (9%)
  between operations  13.5 us (4%)
  other arithmetic  11.9 us (4%)
    all_gather x1, waiting for transfers between devices, per_device(): lax.all_gather(flat_values, 'outer', axis=0, tiled=True)  101 us
    all_gather x1, waiting for transfers between devices, per_device(): lax.all_gather(flat_keys, 'outer', axis=0, tiled=True)  99 us
    all_to_all x1, blocking collectives, per_device(): lax.all_to_all(local_out, 'inner', split_axis=0, concat_axis=2, tiled=True)  29.7 us
    dynamic_slice x48, local copies, waits for them, and re-layouts, attend_piece(): running, unused = lax.scan(one_block, running, (key_blocks, value_blocks))  27.2 us
    dot_general x16, matrix products, attend_keys(): jnp.einsum('qhk,khd->qhd', weights.astype(jnp.bfloat16), value_heads, pre...  18.3 us
    dot_general x16, matrix products, attend_keys(): jnp.einsum('qhd,khd->qhk', query_heads, key_heads, preferred_element_type...  12.4 us
    reduce_sum x16, other arithmetic, attend_keys(): totals = totals * shrink + jnp.sum(weights, axis=2)  11.3 us
  transfers between devices with their start and end apart: 2, of which 2 were waited for; matrix products, arithmetic and copies ran while one was open for 1% of the time, Pallas kernels for 0%

commit v1 on v0

--- a/solution.py
+++ b/solution.py
@@ -6,6 +6,13 @@
 from jax.sharding import PartitionSpec as P
 
 HEAD_DIM = 128
+
+
+def swapped_in(x, axis, dim):
+    peers = lax.axis_size(axis)
+    blocks = jnp.stack([x for _ in range(peers)])
+    blocks = lax.all_to_all(blocks, axis, split_axis=0, concat_axis=0)
+    return jnp.concatenate(blocks, axis=dim)
 
 
 def attend_keys(running, key_block, value_block, query_heads, head_count):
@@ -70,7 +77,7 @@
         start_state(tok_rows, head_count),
         (
             lax.all_gather(flat_keys, "outer", axis=0, tiled=True),
-            lax.all_gather(flat_values, "outer", axis=0, tiled=True),
+            swapped_in(flat_values, "outer", 0),
         ),
         jnp.int32(0),
     )

time: 322 us -> 479 us (1.49); the launches traced: 321 us -> 470 us
  waiting for transfers between devices: 200 us -> 267 us
  other arithmetic: 11.9 us -> 49.4 us
  matrix products: 30.6 us -> 61.5 us
  local copies, waits for them, and re-layouts: 34.4 us -> 47.1 us
  starting transfers between devices: 0.04 us -> 8.65 us
  blocking collectives: 29.7 us -> 22.3 us
    all_to_all x0 -> x1, waiting for transfers between devices: none -> 267 us  [swapped_in(): blocks = lax.all_to_all(blocks, axis, split_axis=0, concat_axis=0)]
    all_gather x1 -> x0, waiting for transfers between devices: 101 us -> none  [per_device(): lax.all_gather(flat_values, 'outer', axis=0, tiled=True)]
    all_gather x1, waiting for transfers between devices: 99 us -> 0.01 us  [per_device(): lax.all_gather(flat_keys, 'outer', axis=0, tiled=True)]
    reduce_sum x16, other arithmetic: 11.3 us -> 48.9 us  [attend_keys(): totals = totals * shrink + jnp.sum(weights, axis=2)]
    dot_general x16, matrix products: 12.4 us -> 43.2 us  [attend_keys(): jnp.einsum('qhd,khd->qhk', query_heads, key_heads, preferred_element_type...]
    dynamic_slice x48, local copies, waits for them, and re-layouts: 27.2 us -> 38 us  [attend_piece(): running, unused = lax.scan(one_block, running, (key_blocks, value_blocks))]
    all_to_all x0 -> x1, starting transfers between devices: none -> 8.61 us  [swapped_in(): blocks = lax.all_to_all(blocks, axis, split_axis=0, concat_axis=0)]
    all_to_all x1, blocking collectives: 29.7 us -> 22.3 us  [per_device(): lax.all_to_all(local_out, 'inner', split_axis=0, concat_axis=2, tiled=True)]
  transfers between devices with their start and end apart: 2 -> 2, of which waited for: 2 -> 1; matrix products, arithmetic and copies ran while one was open for 1% -> 0% of each run, Pallas kernels for 0% -> 0%
where the time goes in v1:
time: 479 us; the launch traced here: 470 us
  waiting for transfers between devices  267 us (56%)
  matrix products  61.5 us (13%)
  other arithmetic  49.4 us (10%)
  local copies, waits for them, and re-layouts  47.1 us (10%)
  blocking collectives  22.3 us (5%)
  between operations  13.5 us (3%)
  starting transfers between devices  8.65 us (2%)
    all_to_all x1, waiting for transfers between devices, swapped_in(): blocks = lax.all_to_all(blocks, axis, split_axis=0, concat_axis=0)  267 us
    reduce_sum x16, other arithmetic, attend_keys(): totals = totals * shrink + jnp.sum(weights, axis=2)  48.9 us
    dot_general x16, matrix products, attend_keys(): jnp.einsum('qhd,khd->qhk', query_heads, key_heads, preferred_element_type...  43.2 us
    dynamic_slice x48, local copies, waits for them, and re-layouts, attend_piece(): running, unused = lax.scan(one_block, running, (key_blocks, value_blocks))  38 us
    all_to_all x1, blocking collectives, per_device(): lax.all_to_all(local_out, 'inner', split_axis=0, concat_axis=2, tiled=True)  22.3 us
    dot_general x16, matrix products, attend_keys(): jnp.einsum('qhk,khd->qhd', weights.astype(jnp.bfloat16), value_heads, pre...  18.3 us
  transfers between devices with their start and end apart: 2, of which 1 were waited for; matrix products, arithmetic and copies ran while one was open for 0% of the time, Pallas kernels for 0%

profile of v1, /device:TPU:32, one launch (start us, length us, event | category | flops | bytes accessed | tf_op | source)
XLA Modules:
  0.0 470.1 jit_solution(4714705554312195685)
XLA Ops:
  6.5 1.3 copy.32
  7.8 4.0 stack.3
  11.9 8.6 %all-to-all-start = ((bf16[16,512,512]{1,2,0:T(8,128)(2,1)}), bf16[16,512,512]{1,2,0:T(8,128)(2,1)}, u32[]{:S(2)}, u32[]{:S(2)}) async-start(bf16[16,512,512]{1,2,0:T(8,128)(2,1)} %stack.3), calls=%async_computation | async-start | bytes 16777216 | tf_op jit(solution)/shard_map/all_to_all | solution.py:14
  22.5 266.6 %all-to-all-done = bf16[16,512,512]{1,2,0:T(8,128)(2,1)} async-done(((bf16[16,512,512]{1,2,0:T(8,128)(2,1)}), bf16[16,512,512]{1,2,0:T(8,128)(2,1)}, u32[]{:S(2)}, u32[]{:S(2)}) %all-to-all-start) | async-done | bytes 8388640 | tf_op jit(solution)/shard_map/all_to_all | solution.py:14
  289.2 149.8 %while.15 = (s32[]{:T(128)}, f32[512,4]{0,1:T(4,128)S(1)}, f32[512,4]{0,1:T(4,128)S(1)}, f32[512,4,128]{0,2,1:T(8,128)S(1)}, bf16[16,512,512]{2,1,0:T(8,128)(2,1...) while((s32[]{:T(128)}, f32[512,4]{0,1:T(4,128)S(1)}, ...), condition=%wide.region_3.4_spmd.clone, body=%wide.region_0.3_spmd.clone.sunk | while | flops 546056192 | bytes 36307084 | solution.py:50
  290.5 2.7 bitcast_reduce_fusion.2
  293.2 3.1 fusion.29
  296.3 1.1 constant_dynamic-slice_fusion.5
  297.4 1.1 fusion.31
  299.8 2.7 bitcast_reduce_fusion.2
  302.5 3.1 fusion.29
  305.6 1.1 constant_dynamic-slice_fusion.5
  306.7 1.1 fusion.31
  309.2 2.7 bitcast_reduce_fusion.2
  311.9 3.1 fusion.29
  315.0 1.1 constant_dynamic-slice_fusion.5
  316.1 1.1 fusion.31
  318.6 2.7 bitcast_reduce_fusion.2
  321.3 3.1 fusion.29
  324.4 1.1 constant_dynamic-slice_fusion.5
  325.5 1.1 fusion.31
  327.9 2.7 bitcast_reduce_fusion.2
  330.6 3.1 fusion.29
  333.7 1.1 constant_dynamic-slice_fusion.5
  334.8 1.1 fusion.31
  337.3 2.7 bitcast_reduce_fusion.2
  340.0 3.1 fusion.29
  343.1 1.1 constant_dynamic-slice_fusion.5
  344.2 1.1 fusion.31
  346.7 2.7 bitcast_reduce_fusion.2
  349.4 3.1 fusion.29
  352.4 1.1 constant_dynamic-slice_fusion.5
  353.5 1.1 fusion.31
  356.0 2.7 bitcast_reduce_fusion.2
  358.7 3.1 fusion.29
  361.8 1.1 constant_dynamic-slice_fusion.5
  362.9 1.1 fusion.31
  365.4 2.7 bitcast_reduce_fusion.2
  368.1 3.1 fusion.29
  371.2 1.1 constant_dynamic-slice_fusion.5
  372.3 1.1 fusion.31
  374.7 2.7 bitcast_reduce_fusion.2
  377.5 3.1 fusion.29
  381.6 1.1 fusion.31
  384.1 2.7 bitcast_reduce_fusion.2
  386.8 3.1 fusion.29
  389.9 1.1 constant_dynamic-slice_fusion.5
  391.0 1.1 fusion.31
  393.5 2.7 bitcast_reduce_fusion.2
  396.2 3.1 fusion.29
  400.4 1.1 fusion.31
  402.8 2.7 bitcast_reduce_fusion.2
  405.6 3.1 fusion.29
  409.7 1.1 fusion.31
  412.2 2.7 bitcast_reduce_fusion.2
  414.9 3.1 fusion.29
  419.1 1.1 fusion.31
  421.6 2.7 bitcast_reduce_fusion.2
  424.3 3.1 fusion.29
  428.5 1.1 fusion.31
  430.9 2.7 bitcast_reduce_fusion.2
  433.6 3.1 fusion.29
  437.8 1.1 fusion.31
  439.6 22.3 %all_to_all.23 = bf16[512,2,256]{2,1,0:T(2,128)(2,1)S(1)} all-to-all(bf16[512,2,256]{2,1,0:T(2,128)(2,1)S(1)} %copy.26), channel_id=1, replica_groups=mesh['outer'=16,'inner'=16] {'inner'}, dimensions={0} | all-to-all | bytes 1048576 | tf_op jit(solution)/shard_map/all_to_all | solution.py:85
  (136 shorter events, 31.5 us)
Async XLA Ops:
  11.9 8.7 %copy-start.1 = (bf16[512,2,256]{2,1,0:T(2,128)(2,1)S(1)}, bf16[512,2,256]{2,1,0:T(2,128)(2,1)}, u32[]{:S(2)}) copy-start(bf16[512,2,256]{2,1,0:T(2,128)(2,1)} %param.6) | copy-start | bytes 1572868
  11.9 9.6 %copy-start.2 = (bf16[512,2,256]{2,1,0:T(2,128)(2,1)S(1)}, bf16[512,2,256]{2,1,0:T(2,128)(2,1)}, u32[]{:S(2)}) copy-start(bf16[512,2,256]{2,1,0:T(2,128)(2,1)} %param.5) | copy-start | bytes 1572868
  11.9 277.3 %all-to-all-start = ((bf16[16,512,512]{1,2,0:T(8,128)(2,1)}), bf16[16,512,512]{1,2,0:T(8,128)(2,1)}, u32[]{:S(2)}, u32[]{:S(2)}) async-start(bf16[16,512,512]{1,2,0:T(8,128)(2,1)} %stack.3), calls=%async_computation | async-start | bytes 16777216 | tf_op jit(solution)/shard_map/all_to_all | solution.py:14
  20.5 268.7 %all-gather.2.cloned.1.call-start = ((), (), s32[]{:S(2)}) async-start(), calls=%async_computation.2 | async-start | bytes 8912896 | tf_op jit(solution)/shard_map/all_gather | solution.py:79
  293.2 4.2 copy-start
  302.5 4.2 copy-start
  311.9 4.2 copy-start
  321.3 4.2 copy-start
  330.6 4.2 copy-start
  340.0 4.2 copy-start
  349.4 4.2 copy-start
  358.7 4.2 copy-start
  368.1 4.2 copy-start
  377.5 4.2 copy-start
  386.8 4.2 copy-start
  396.2 4.2 copy-start
  405.5 4.2 copy-start
  414.9 4.2 copy-start
  424.3 4.2 copy-start
  433.6 4.2 copy-start
Sparse Core Ops, SparseCore 0:
  23.1 245.1 all-gather.1

commit v2 on v0

--- a/solution.py
+++ b/solution.py
@@ -75,7 +75,10 @@
         jnp.int32(0),
     )
     local_out = finish_state(running).reshape(tok_rows, networks, local_cols)
-    attended = lax.all_to_all(local_out, "inner", split_axis=0, concat_axis=2, tiled=True)
+    n_dev = lax.axis_size("inner")
+    parts = jnp.stack(jnp.split(local_out, n_dev, axis=0), axis=0)
+    parts = lax.all_to_all(parts, "inner", split_axis=0, concat_axis=0)
+    attended = jnp.concatenate(parts, axis=2)
     return attended
 
 

time: 322 us -> 324 us (level)
  no operation moved by 1% of the time
where the time goes in v2:
time: 324 us; the launch traced here: 323 us
  waiting for transfers between devices  200 us (62%)
  local copies, waits for them, and re-layouts  36.8 us (11%)
  matrix products  30.6 us (9%)
  blocking collectives  29.7 us (9%)
  between operations  13.6 us (4%)
  other arithmetic  11.9 us (4%)
    all_gather x1, waiting for transfers between devices, per_device(): lax.all_gather(flat_values, 'outer', axis=0, tiled=True)  101 us
    all_gather x1, waiting for transfers between devices, per_device(): lax.all_gather(flat_keys, 'outer', axis=0, tiled=True)  99 us
    all_to_all x1, blocking collectives, per_device(): parts = lax.all_to_all(parts, 'inner', split_axis=0, concat_axis=0)  29.7 us
    dynamic_slice x48, local copies, waits for them, and re-layouts, attend_piece(): running, unused = lax.scan(one_block, running, (key_blocks, value_blocks))  27.2 us
    dot_general x16, matrix products, attend_keys(): jnp.einsum('qhk,khd->qhd', weights.astype(jnp.bfloat16), value_heads, pre...  18.3 us
    dot_general x16, matrix products, attend_keys(): jnp.einsum('qhd,khd->qhk', query_heads, key_heads, preferred_element_type...  12.4 us
    reduce_sum x16, other arithmetic, attend_keys(): totals = totals * shrink + jnp.sum(weights, axis=2)  11.3 us
  transfers between devices with their start and end apart: 2, of which 2 were waited for; matrix products, arithmetic and copies ran while one was open for 1% of the time, Pallas kernels for 0%

profile of v2, /device:TPU:32, one launch (start us, length us, event | category | flops | bytes accessed | tf_op | source)
XLA Modules:
  0.0 323.5 jit_solution(6103479896864559688)
XLA Ops:
  6.5 1.9 copy.133
  8.5 1.9 copy.134
  10.5 1.3 copy.88
  12.1 99.0 %all-gather.3.cloned.1.call-done = bf16[8192,512]{1,0:T(8,128)(2,1)} async-done(((bf16[512,512]{1,0:T(8,128)(2,1)}), bf16[8192,512]{1,0:T(8,128)(2,1)}) %all-gather.3.cloned.1.call-update) | async-done | bytes 8388624 | tf_op jit(solution)/shard_map/all_gather | solution.py:72
  111.1 101.0 %all-gather.5.cloned.1.call-done = bf16[8192,512]{1,0:T(8,128)(2,1)} async-done(((bf16[512,512]{1,0:T(8,128)(2,1)}), bf16[8192,512]{1,0:T(8,128)(2,1)}) %all-gather.5.cloned.1.call-update) | async-done | bytes 8388624 | tf_op jit(solution)/shard_map/all_gather | solution.py:73
  212.0 70.4 %while.15 = (s32[]{:T(128)}, f32[512,4]{0,1:T(4,128)S(1)}, f32[512,4]{0,1:T(4,128)S(1)}, f32[512,4,128]{0,2,1:T(8,128)S(1)}, bf16[16,512,512]{2,1,0:T(8,128)(2,1...) while((s32[]{:T(128)}, f32[512,4]{0,1:T(4,128)S(1)}, ...), condition=%wide.region_3.4_spmd.clone, body=%wide.region_0.3_spmd.clone.sunk | while | flops 546056192 | bytes 20578420 | solution.py:43
  212.0 1.3 constant_dynamic-slice_fusion.3
  213.7 0.8 bitcast_reduce_fusion.2
  214.5 0.7 fusion.30
  215.2 1.1 fusion.32
  216.4 1.3 constant_dynamic-slice_fusion.3
  218.1 0.8 bitcast_reduce_fusion.2
  218.9 0.7 fusion.30
  219.6 1.1 fusion.32
  220.8 1.3 constant_dynamic-slice_fusion.3
  222.5 0.8 bitcast_reduce_fusion.2
  223.3 0.7 fusion.30
  224.1 1.1 fusion.32
  225.2 1.3 constant_dynamic-slice_fusion.3
  226.9 0.8 bitcast_reduce_fusion.2
  227.7 0.7 fusion.30
  228.5 1.1 fusion.32
  229.6 1.3 constant_dynamic-slice_fusion.3
  231.3 0.8 bitcast_reduce_fusion.2
  232.1 0.7 fusion.30
  232.9 1.1 fusion.32
  234.0 1.3 constant_dynamic-slice_fusion.3
  235.7 0.8 bitcast_reduce_fusion.2
  237.3 1.1 fusion.32
  238.4 1.3 constant_dynamic-slice_fusion.3
  240.2 0.8 bitcast_reduce_fusion.2
  240.9 0.7 fusion.30
  241.7 1.1 fusion.32
  242.8 1.3 constant_dynamic-slice_fusion.3
  244.6 0.8 bitcast_reduce_fusion.2
  246.1 1.1 fusion.32
  247.3 1.3 constant_dynamic-slice_fusion.3
  249.0 0.8 bitcast_reduce_fusion.2
  249.7 0.7 fusion.30
  250.5 1.1 fusion.32
  251.7 1.3 constant_dynamic-slice_fusion.3
  253.4 0.8 bitcast_reduce_fusion.2
  254.9 1.1 fusion.32
  256.1 1.3 constant_dynamic-slice_fusion.3
  257.8 0.8 bitcast_reduce_fusion.2
  258.6 0.7 fusion.30
  259.3 1.1 fusion.32
  260.5 1.3 constant_dynamic-slice_fusion.3
  262.2 0.8 bitcast_reduce_fusion.2
  263.7 1.1 fusion.32
  264.9 1.3 constant_dynamic-slice_fusion.3
  266.6 0.8 bitcast_reduce_fusion.2
  268.1 1.1 fusion.32
  269.3 1.3 constant_dynamic-slice_fusion.3
  271.0 0.8 bitcast_reduce_fusion.2
  272.5 1.1 fusion.32
  273.7 1.3 constant_dynamic-slice_fusion.3
  275.4 0.8 bitcast_reduce_fusion.2
  276.9 1.1 fusion.32
  278.1 1.3 constant_dynamic-slice_fusion.3
  279.8 0.8 bitcast_reduce_fusion.2
  281.3 1.1 fusion.32
  285.6 29.7 %all_to_all.5 = bf16[16,32,2,256]{3,2,1,0:T(2,128)(2,1)S(1)} all-to-all(bf16[16,32,2,256]{3,2,1,0:T(2,128)(2,1)S(1)} %constant_dynamic-update-slice_fusion), channel_id=1, replica_groups=mesh['outer'=16,'inner'=16] {'inner'}, dimensions={0} | all-to-all | bytes 1048576 | tf_op jit(solution)/shard_map/all_to_all | solution.py:80
  315.3 1.4 copy.132
  (130 shorter events, 16.2 us)
Async XLA Ops:
  6.5 104.5 %all-gather.3.cloned.1.call-start = ((), (), s32[]{:S(2)}) async-start(), calls=%async_computation.1 | async-start | bytes 8912896 | tf_op jit(solution)/shard_map/all_gather | solution.py:72
  8.5 203.5 %all-gather.5.cloned.1.call-start = ((), (), s32[]{:S(2)}) async-start(), calls=%async_computation.2 | async-start | bytes 8912896 | tf_op jit(solution)/shard_map/all_gather | solution.py:73
Sparse Core Ops, SparseCore 0:
  9.1 101.9 all-gather.2
  112.9 99.1 all-gather.4
